TPU v7x, 32 devices: a whole 2x2x4 slice. The times are simulated.
32 devices in a mesh: owner: 4 (over z), slab: 2 (over y), red: 4 (over x, core).
Axes of the slice: x: 2, y: 2, z: 4, core: 2. Of those that a mesh axis runs over, the one named last changes fastest.
Arguments:
- amplitudes: bfloat16 [64, 128, 256], P(('owner', 'slab', 'red')), may hold values from -6 to 6
- integrals: bfloat16 [32, 128, 128], P('slab'), may hold values from -0.21875 to 0.21875
- requests: int32 [4, 2, 4, 4], P('owner', 'slab', 'red'), may hold values from 0 to 1
- task_slot: int32 [4, 2, 4, 8, 12], P('owner', 'slab', 'red'), may hold values from 0 to 3
- task_integral: int32 [4, 2, 4, 8, 12], P('owner', 'slab', 'red'), may hold values from 0 to 31
- live_tasks: int32 [4, 2, 4], P('owner', 'slab', 'red'), may hold values from 3 to 12, as said below
- denominators: float32 [64, 128, 256], P(('owner', 'slab', 'red')), may hold values from 0.5 to 5
Outputs:
- update: float32 [64, 128, 256], P(('owner', 'slab', 'red'))
Inputs may be any that keep to these rules, and one draw needn't show every extreme that they name: `live_tasks`: slots below a device's count are live; in every draw some devices have all 12 live.
All inputs are finite; a program needn't handle non-finite values.
Results may differ from a plain program's by a relative error of at most 0.0003.
Values may be sent and summed in bfloat16 or wider, within the bound.
A program may use at most 64 MiB of HBM per device.

v0:
```python
import jax
import jax.numpy as jnp
from jax import lax
from jax.sharding import PartitionSpec as P


def on_device(amplitudes, integrals, requests, task_slot, task_integral, live_tasks, denominators):
    owners = lax.axis_size("owner")
    per_owner = amplitudes.shape[0]
    wanted = requests.reshape(owners)
    every_tile = lax.all_gather(amplitudes, "owner", axis=0, tiled=True)
    global_index = jnp.arange(owners, dtype=jnp.int32) * per_owner + wanted
    pulled = jnp.take(every_tile, global_index, axis=0)
    gathered_integrals = lax.all_gather(integrals, "slab", axis=0, tiled=True)
    group_tiles = task_slot.shape[3]
    slot_count = task_slot.shape[4]
    slot_table = task_slot.reshape(group_tiles, slot_count)
    integral_table = task_integral.reshape(group_tiles, slot_count)
    live_count = live_tasks.reshape(())
    slot_width = 4
    tile_rows = amplitudes.shape[1]
    tile_columns = amplitudes.shape[2]

    def accumulate(block_index, partial_value):
        first_slot = block_index * slot_width
        slot_block = lax.dynamic_slice_in_dim(slot_table, first_slot, slot_width, 1)
        integral_block = lax.dynamic_slice_in_dim(integral_table, first_slot, slot_width, 1)
        live_mask = (first_slot + jnp.arange(slot_width, dtype=jnp.int32) < live_count).astype(
            jnp.bfloat16
        )
        integral_rows = (
            jnp.take(gathered_integrals, integral_block, axis=0) * live_mask[None, :, None, None]
        )
        amplitude_rows = jnp.take(pulled, slot_block, axis=0)
        return partial_value + jnp.einsum(
            "qkac,qkcx->qax", integral_rows, amplitude_rows, preferred_element_type=jnp.float32
        )

    blocks_live = (live_count + slot_width - 1) // slot_width
    initial = jnp.zeros((group_tiles, tile_rows, tile_columns), jnp.float32)
    partial_value = lax.fori_loop(0, blocks_live, accumulate, initial)
    residual = lax.psum_scatter(partial_value, "red", scatter_dimension=0, tiled=True)
    return residual / denominators


def solution(mesh):
    placed = (
        P(("owner", "slab", "red"), None, None),
        P("slab", None, None),
        P("owner", "slab", "red", None),
        P("owner", "slab", "red", None, None),
        P("owner", "slab", "red", None, None),
        P("owner", "slab", "red"),
        P(("owner", "slab", "red"), None, None),
    )
    return jax.shard_map(
        on_device,
        mesh=mesh,
        in_specs=placed,
        out_specs=P(("owner", "slab", "red"), None, None),
        check_vma=False,
    )
```

profile of v0, /device:TPU:1, one launch (start us, length us, event | category | flops | bytes accessed | tf_op | source)
XLA Modules:
  0.0 84.7 jit_solution(17166635921086269410)
XLA Ops:
  6.5 0.0 copy-start
  6.5 0.0 copy-start.1
  6.5 0.0 all-gather.2.cloned.1.call-start
  6.5 0.7 all-gather.2.cloned.1.call-update
  7.3 0.0 reduce-scatter.2.cloned.1.call-start
  8.0 0.7 fusion.16
  8.6 15.5 %all_gather.7 = bf16[8,128,256]{2,1,0:T(8,128)(2,1)S(1)} all-gather(bf16[2,128,256]{2,1,0:T(8,128)(2,1)} %param.9), channel_id=1, replica_groups=mesh['owner'=4,'slab'=2,'red'=4] {'owner'}, dimensions={0}, use_global_device_ids=true | all-gather | bytes 655360 | tf_op jit(solution)/shard_map/all_gather | solution.py:11
  24.2 0.6 gather_fusion.2
  24.8 0.7 compare_and_fusion.2
  25.4 0.1 broadcast_select_fusion
  25.5 6.6 %all-gather.2.cloned.1.call-done = bf16[32,128,128]{2,1,0:T(8,128)(2,1)} async-done(((bf16[16,128,128]{2,1,0:T(8,128)(2,1)}), bf16[32,128,128]{2,1,0:T(8,128)(2,1)}) %all-gather.2.cloned.1.call-update) | async-done | bytes 1048592 | tf_op jit(solution)/shard_map/all_gather | solution.py:14
  32.1 1.1 %broadcast_in_dim.38 = f32[8,128,256]{2,1,0:T(8,128)} broadcast(f32[]{:T(128)} %constant.66.clone.1), dimensions={} | broadcast | bytes 1048580 | tf_op jit(solution)/shard_map/broadcast_in_dim | solution.py:40
  33.2 0.0 copy-done
  33.2 0.0 copy-done.1
  33.2 6.5 %while.10 = (s32[]{:T(128)}, f32[8,128,256]{2,1,0:T(8,128)}, s32[]{:T(128)}, s32[8,12]{1,0:T(8,128)S(1)}, bf16[32,128,128]{2,1,0:T(8,128)(2,1)}, /*index=5*/s32[...) while((s32[]{:T(128)}, f32[8,128,256]{2,1,0:T(8,128)}, ...), condition=%wide.region_1.2_spmd, body=%wide.region_0.1_spmd.sunk | while | flops 270797216 | bytes 11544383 | solution.py:41
  33.2 0.7 compare_convert_fusion.2
  33.9 0.1 compare_and_fusion.4
  34.0 0.1 reshape.107
  34.0 0.1 reshape.108
  34.1 2.0 %gather_fusion.1 = bf16[32,128,128]{2,1,0:T(8,128)(2,1)S(1)} fusion(bf16[32,128,128]{2,1,0:T(8,128)(2,1)} %get-tuple-element.157, s32[1024]{0:T(1024)S(1)} %pad_clamp_fusion.6), kind=kCustom, calls=%fused_computation.clone.1 | custom fusion | bytes 2097280 | tf_op jit(solution)/shard_map/while/body/jit(_take)/gather | solution.py:32
  36.1 0.7 gather_fusion
  36.8 2.9 %fusion.22 = f32[8,128,256]{2,1,0:T(8,128)} fusion(f32[8,128,256]{2,1,0:T(8,128)} %get-tuple-element.142, bf16[8,4,128,256]{3,2,1,0:T(8,128)(2,1)S(1)} %bitcast.27, pred[8,4]{1,0:T(8,128)(4,1)S(1)} %get-tuple-element.126, bf16[8,4,128,128]{3,2,1,0:T(8,128)(2,1)S(1)} %bitcast.28, pred[8,4]{1,0:T(8,128)(4,1)S(1)} %get-tuple-element.128, ...), kind=kOutput, calls=%fused_computation.7.clone.1 | convolution fusion | flops 270794752 | bytes 5242952 | tf_op jit(solution)/shard_map/while/body/qkac,qkcx->qax/dot_general | solution.py:35
  39.7 0.0 reduce-scatter.2.cloned.1.call-update
  39.7 36.3 %reduce-scatter.2.cloned.1.call-done = f32[2,128,256]{2,1,0:T(8,128)} async-done(((f32[8,128,256]{2,1,0:T(8,128)}), f32[2,128,256]{2,1,0:T(8,128)}) %reduce-scatter.2.cloned.1.call-update) | async-done | bytes 262160 | tf_op jit(solution)/shard_map/reduce_scatter | solution.py:42
  76.1 1.8 %div.14 = f32[2,128,256]{2,1,0:T(8,128)} divide(f32[2,128,256]{2,1,0:T(8,128)} %reduce-scatter.2.cloned.1.call-done, f32[2,128,256]{2,1,0:T(8,128)} %param.15) | non-fusion elementwise | flops 65536 | bytes 786432 | tf_op jit(solution)/shard_map/div | solution.py:43
  (3 shorter events, 0.0 us)
Async XLA Ops:
  6.5 26.7 %copy-start = (s32[1,1,1,8,12]{4,3,2,1,0:T(8,128)S(1)}, s32[1,1,1,8,12]{4,3,2,1,0:T(8,128)}, u32[]{:S(2)}) copy-start(s32[1,1,1,8,12]{4,3,2,1,0:T(8,128)} %param.13) | copy-start | bytes 1156
  6.5 26.7 %copy-start.1 = (s32[1,1,1,8,12]{4,3,2,1,0:T(8,128)S(1)}, s32[1,1,1,8,12]{4,3,2,1,0:T(8,128)}, u32[]{:S(2)}) copy-start(s32[1,1,1,8,12]{4,3,2,1,0:T(8,128)} %param.12) | copy-start | bytes 1156
  6.5 25.6 %all-gather.2.cloned.1.call-start = ((), (), s32[]{:S(2)}) async-start(), calls=%async_computation.1 | async-start | bytes 1572864 | tf_op jit(solution)/shard_map/all_gather | solution.py:14
  7.3 68.8 %reduce-scatter.2.cloned.1.call-start = ((), (), s32[]{:S(2)}) async-start(), calls=%async_computation.2 | async-start | bytes 1310720 | tf_op jit(solution)/shard_map/reduce_scatter | solution.py:42
Sparse Core Ops, SparseCore 0:
  8.9 23.1 all-gather.1
  39.9 36.1 reduce-scatter.1
where the time goes:
time: 85.2 us; the launch traced here: 84.7 us
  waiting for transfers between devices  43.6 us (51%)
  blocking collectives  15.5 us (18%)
  between operations  14.1 us (17%)
  local copies, waits for them, and re-layouts  4.5 us (5%)
  other arithmetic  3.95 us (5%)
  matrix products  2.9 us (3%)
    reduce_scatter x1, waiting for transfers between devices, on_device(): lax.psum_scatter(partial_value, 'red', scatter_dimension=0, tiled=True)  36.3 us
    all_gather x1, blocking collectives, on_device(): every_tile = lax.all_gather(amplitudes, 'owner', axis=0, tiled=True)  15.5 us
    all_gather x1, waiting for transfers between devices, on_device(): gathered_integrals = lax.all_gather(integrals, 'slab', axis=0, tiled=True)  6.57 us
    dot_general x1, matrix products, accumulate(): jnp.einsum('qkac,qkcx->qax', integral_rows, amplitude_rows, preferred_ele...  2.9 us
    gather x1, local copies, waits for them, and re-layouts, accumulate(): jnp.take(gathered_integrals, integral_block, axis=0)  1.97 us
    div x1, other arithmetic, on_device(): return residual / denominators  1.77 us
  transfers between devices with their start and end apart: 2, of which 2 were waited for; matrix products, arithmetic and copies ran while one was open for 2% of the time, Pallas kernels for 0%

commit v1 on v0

v1 whole, which is shorter than its diff:
```python
import functools

import jax
import jax.numpy as jnp
from jax import lax
from jax.experimental import pallas as pl
from jax.experimental.pallas import tpu as pltpu
from jax.sharding import PartitionSpec as P

MESH = pl.DeviceIdType.MESH
CORES = 2
INT_CHUNKS = 2


def kernel(sizes, amp_hbm, int_hbm, req_hbm, slot_hbm, task_hbm, live_hbm, out_ref, *scratch):
    owners, slabs, reds, per_owner, int_local, group_tiles, slots = sizes
    chips = reds // CORES
    keep = group_tiles // reds
    (mine, ints, below, above, stage, own, part) = scratch[:7]
    far = scratch[7 : 7 + 2 * (chips - 1)]
    (req_v, slot_v, task_v, live_v, my_req_s, req_s, slot_s, task_s, live_s,
     local_sem, req_send, req_recv, tab_send, tab_recv, near_send, near_recv, z_send, z_recv,
     int_send, int_recv, intf_send, intf_recv, part_send, part_recv,
     x_send, x_recv, f_send, f_recv) = scratch[7 + 2 * (chips - 1):]
    o = lax.axis_index("owner")
    s = lax.axis_index("slab")
    r = lax.axis_index("red")
    chip = r // CORES
    core = r % CORES
    mate = chip * CORES + (1 - core)

    def rcopy(src, dst, send, recv, **where):
        return pltpu.make_async_remote_copy(
            src_ref=src, dst_ref=dst, send_sem=send, recv_sem=recv, device_id=where, device_id_type=MESH
        )

    local = [
        pltpu.make_async_copy(req_hbm, req_v.at[o], local_sem.at[0]),
        pltpu.make_async_copy(req_hbm, my_req_s, local_sem.at[1]),
        pltpu.make_async_copy(amp_hbm, mine, local_sem.at[2]),
        pltpu.make_async_copy(int_hbm, ints.at[pl.ds(s * int_local, int_local)], local_sem.at[3]),
        pltpu.make_async_copy(slot_hbm, slot_v.at[r], local_sem.at[4]),
        pltpu.make_async_copy(task_hbm, task_v.at[r], local_sem.at[5]),
        pltpu.make_async_copy(live_hbm, live_v.at[r], local_sem.at[6]),
    ]
    for copy in local:
        copy.start()

    barrier = pltpu.get_barrier_semaphore()
    for d in range(1, owners):
        pl.semaphore_signal(barrier, inc=1, device_id={"owner": lax.rem(o + d, owners)}, device_id_type=MESH)
    for d in range(1, slabs):
        pl.semaphore_signal(barrier, inc=1, device_id={"slab": lax.rem(s + d, slabs)}, device_id_type=MESH)
    for d in range(1, reds):
        pl.semaphore_signal(barrier, inc=1, device_id={"red": lax.rem(r + d, reds)}, device_id_type=MESH)
    dead = slabs * int_local
    ints[dead] = jnp.zeros(ints.shape[1:], ints.dtype)
    for copy in local:
        copy.wait()
    pl.semaphore_wait(barrier, owners - 1 + slabs - 1 + reds - 1)

    def is_near(q):
        return jnp.abs(q - o) == 1

    def is_far(q):
        return jnp.abs(q - o) > 1

    for q in range(owners):
        @pl.when(q != o)
        def _():
            rcopy(req_v.at[o], req_v.at[o], req_send.at[q], req_recv.at[o], owner=q).start()

    def to_neighbours(act):
        @pl.when(o + 1 < owners)
        def _():
            act(rcopy(mine, below, near_send.at[0], near_recv.at[0], owner=jnp.minimum(o + 1, owners - 1)))

        @pl.when(o > 0)
        def _():
            act(rcopy(mine, above, near_send.at[1], near_recv.at[1], owner=jnp.maximum(o - 1, 0)))

    to_neighbours(lambda copy: copy.start())

    def spread(p):
        for dx in range(1, chips):
            there = lax.rem(chip + chips - dx, chips) * CORES + core
            rcopy(own.at[p], far[2 * (dx - 1)].at[p], x_send.at[dx - 1, p], x_recv.at[dx - 1, p], red=there).start()
        rcopy(own.at[p], part.at[p], part_send.at[p], part_recv.at[p], red=mate).start()

    def forward(p):
        for dx in range(1, chips):
            a, b = far[2 * (dx - 1)], far[2 * (dx - 1) + 1]
            rcopy(own.at[p], a.at[p], x_send.at[dx - 1, p], x_recv.at[dx - 1, p], red=mate).wait_recv()
            rcopy(a.at[p], b.at[p], f_send.at[dx - 1, p], f_recv.at[dx - 1, p], red=mate).start()

    own[o] = mine[my_req_s[0, o]]

    half = int_local // CORES
    chunk = half // INT_CHUNKS

    def int_part(slab, which, j):
        return ints.at[pl.ds(slab * int_local + which * half + j * chunk, chunk)]

    for j in range(INT_CHUNKS):
        for d in range(1, slabs):
            rcopy(int_part(s, core, j), int_part(s, core, j), int_send.at[d - 1, j], int_recv.at[d - 1, j],
                  slab=lax.rem(s + d, slabs)).start()

    tables = (slot_v, task_v, live_v)
    for d in range(1, reds):
        for t, ref in enumerate(tables):
            rcopy(ref.at[r], ref.at[r], tab_send.at[d - 1, t], tab_recv.at[d - 1, t],
                  red=lax.rem(r + d, reds)).start()

    for q in range(owners):
        @pl.when(q != o)
        def _():
            rcopy(req_v.at[q], req_v.at[q], req_send.at[q], req_recv.at[q], owner=q).wait_recv()
    to_smem = pltpu.make_async_copy(req_v, req_s, local_sem.at[0])
    to_smem.start()
    spread(o)
    to_smem.wait()
    for q in range(owners):
        @pl.when(is_far(q))
        def _():
            stage[q] = mine[req_s[q, 0, o]]
    for q in range(owners):
        @pl.when(is_far(q))
        def _():
            rcopy(stage.at[q], own.at[o], z_send.at[q], z_recv.at[o], owner=q).start()

    for d in range(1, reds):
        for t, ref in enumerate(tables):
            there = lax.rem(r + reds - d, reds)
            rcopy(ref.at[there], ref.at[there], tab_send.at[d - 1, t], tab_recv.at[d - 1, t], red=there).wait_recv()
    table_copies = [
        pltpu.make_async_copy(ref, to, local_sem.at[1 + t])
        for t, (ref, to) in enumerate(zip(tables, (slot_s, task_s, live_s)))
    ]
    for copy in table_copies:
        copy.start()

    for p in range(owners):
        for side, ref, here in ((0, below, o - 1), (1, above, o + 1)):
            @pl.when(here == p)
            def _():
                rcopy(mine, ref, near_send.at[side], near_recv.at[side], owner=p).wait_recv()
                own[p] = ref[my_req_s[0, p]]
                spread(p)

    forward(o)

    def int_forward(d, j):
        slab = lax.rem(s + slabs - d, slabs)
        rcopy(int_part(slab, core, j), int_part(slab, core, j), int_send.at[d - 1, j], int_recv.at[d - 1, j],
              slab=slab).wait_recv()
        rcopy(int_part(slab, core, j), int_part(slab, core, j), intf_send.at[d - 1, j], intf_recv.at[d - 1, j],
              red=mate).start()

    for j in range(INT_CHUNKS):
        for d in range(1, slabs):
            int_forward(d, j)

    for p in range(owners):
        @pl.when(is_near(p))
        def _():
            forward(p)

    for p in range(owners):
        @pl.when(is_far(p))
        def _():
            rcopy(stage.at[p], own.at[p], z_send.at[p], z_recv.at[p], owner=p).wait_recv()
            spread(p)

    for copy in table_copies:
        copy.wait()
    for j in range(INT_CHUNKS):
        for d in range(1, slabs):
            slab = lax.rem(s + slabs - d, slabs)
            rcopy(int_part(slab, 1 - core, j), int_part(slab, 1 - core, j), intf_send.at[d - 1, j],
                  intf_recv.at[d - 1, j], red=mate).wait_recv()

    def contract(member, tiles, first):
        live = live_s[member, 0, 0]
        for q in range(keep):
            row = r * keep + q
            lhs, rhs = [], []
            for k in range(slots):
                which = jnp.where(k < live, task_s[member, row, k], dead)
                lhs.append(ints[which])
                rhs.append(tiles[slot_s[member, row, k]])
            product = jnp.dot(
                jnp.concatenate(lhs, axis=1), jnp.concatenate(rhs, axis=0), preferred_element_type=jnp.float32
            )
            if first:
                out_ref[q] = product
            else:
                out_ref[q] = out_ref[q] + product

    contract(r, own, True)

    for p in range(owners):
        @pl.when(is_far(p))
        def _():
            forward(p)
    for p in range(owners):
        rcopy(own.at[p], part.at[p], part_send.at[p], part_recv.at[p], red=mate).wait_recv()
    contract(mate, part, False)
    for dx in range(1, chips):
        there = lax.rem(chip + dx, chips)
        contract(there * CORES + core, far[2 * (dx - 1)], False)
        for p in range(owners):
            a, b = far[2 * (dx - 1)], far[2 * (dx - 1) + 1]
            rcopy(a.at[p], b.at[p], f_send.at[dx - 1, p], f_recv.at[dx - 1, p], red=mate).wait_recv()
        contract(there * CORES + (1 - core), far[2 * (dx - 1) + 1], False)

    to_neighbours(lambda copy: copy.wait_send())
    for q in range(owners):
        @pl.when(is_far(q))
        def _():
            rcopy(stage.at[q], own.at[o], z_send.at[q], z_recv.at[o], owner=q).wait_send()

        @pl.when(q != o)
        def _():
            rcopy(req_v.at[o], req_v.at[o], req_send.at[q], req_recv.at[o], owner=q).wait_send()

        for dx in range(1, chips):
            a, b = far[2 * (dx - 1)], far[2 * (dx - 1) + 1]
            rcopy(own.at[q], a.at[q], x_send.at[dx - 1, q], x_recv.at[dx - 1, q], red=mate).wait_send()
            rcopy(a.at[q], b.at[q], f_send.at[dx - 1, q], f_recv.at[dx - 1, q], red=mate).wait_send()
        rcopy(own.at[q], part.at[q], part_send.at[q], part_recv.at[q], red=mate).wait_send()
    for j in range(INT_CHUNKS):
        for d in range(1, slabs):
            to = lax.rem(s + d, slabs)
            frm = lax.rem(s + slabs - d, slabs)
            rcopy(int_part(s, core, j), int_part(s, core, j), int_send.at[d - 1, j], int_recv.at[d - 1, j],
                  slab=to).wait_send()
            rcopy(int_part(frm, core, j), int_part(frm, core, j), intf_send.at[d - 1, j], intf_recv.at[d - 1, j],
                  red=mate).wait_send()
    for d in range(1, reds):
        for t, ref in enumerate(tables):
            rcopy(ref.at[r], ref.at[r], tab_send.at[d - 1, t], tab_recv.at[d - 1, t],
                  red=lax.rem(r + d, reds)).wait_send()


def on_device(sizes, amplitudes, integrals, requests, task_slot, task_integral, live_tasks, denominators):
    owners, slabs, reds = sizes
    per_owner, rows, columns = amplitudes.shape
    int_local, int_rows, int_columns = integrals.shape
    group_tiles, slots = task_slot.shape[3:]
    chips = reds // CORES
    keep = group_tiles // reds
    bf16, i32 = amplitudes.dtype, jnp.int32
    tile_set = pltpu.VMEM((owners, rows, columns), bf16)
    dma = pltpu.SemaphoreType.DMA
    scratch = (
        [
            pltpu.VMEM((per_owner, rows, columns), bf16),
            pltpu.VMEM((slabs * int_local + 1, int_rows, int_columns), bf16),
            pltpu.VMEM((per_owner, rows, columns), bf16),
            pltpu.VMEM((per_owner, rows, columns), bf16),
            tile_set,
            tile_set,
            tile_set,
        ]
        + [tile_set] * (2 * (chips - 1))
        + [
            pltpu.VMEM((owners, 1, owners), i32),
            pltpu.VMEM((reds, group_tiles, slots), i32),
            pltpu.VMEM((reds, group_tiles, slots), i32),
            pltpu.VMEM((reds, 1, 1), i32),
            pltpu.SMEM((1, owners), i32),
            pltpu.SMEM((owners, 1, owners), i32),
            pltpu.SMEM((reds, group_tiles, slots), i32),
            pltpu.SMEM((reds, group_tiles, slots), i32),
            pltpu.SMEM((reds, 1, 1), i32),
            dma((7,)),
            dma((owners,)), dma((owners,)),
            dma((reds - 1, 3)), dma((reds - 1, 3)),
            dma((2,)), dma((2,)),
            dma((owners,)), dma((owners,)),
            dma((slabs - 1, INT_CHUNKS)), dma((slabs - 1, INT_CHUNKS)),
            dma((slabs - 1, INT_CHUNKS)), dma((slabs - 1, INT_CHUNKS)),
            dma((owners,)), dma((owners,)),
            dma((chips - 1, owners)), dma((chips - 1, owners)),
            dma((chips - 1, owners)), dma((chips - 1, owners)),
        ]
    )
    whole = (owners, slabs, reds, per_owner, int_local, group_tiles, slots)
    residual = pl.pallas_call(
        functools.partial(kernel, whole),
        out_shape=jax.ShapeDtypeStruct((keep, rows, columns), jnp.float32),
        in_specs=[pl.BlockSpec(memory_space=pl.ANY)] * 6,
        out_specs=pl.BlockSpec(memory_space=pltpu.VMEM),
        scratch_shapes=scratch,
        compiler_params=pltpu.CompilerParams(collective_id=0, has_side_effects=True),
        name="gather_contract",
    )(
        amplitudes,
        integrals,
        requests.reshape(1, owners),
        task_slot.reshape(group_tiles, slots),
        task_integral.reshape(group_tiles, slots),
        live_tasks.reshape(1, 1),
    )
    return residual / denominators


def solution(mesh):
    placed = (
        P(("owner", "slab", "red"), None, None),
        P("slab", None, None),
        P("owner", "slab", "red", None),
        P("owner", "slab", "red", None, None),
        P("owner", "slab", "red", None, None),
        P("owner", "slab", "red"),
        P(("owner", "slab", "red"), None, None),
    )
    sizes = (mesh.shape["owner"], mesh.shape["slab"], mesh.shape["red"])
    return jax.shard_map(
        functools.partial(on_device, sizes),
        mesh=mesh,
        in_specs=placed,
        out_specs=P(("owner", "slab", "red"), None, None),
        check_vma=False,
    )
```

time: 85.2 us -> 22.3 us (0.26)
  waiting for transfers between devices: 43.6 us -> 0 us
  Pallas kernels: 0 us -> 19.8 us
  blocking collectives: 15.5 us -> 0 us
  between operations: 14.1 us -> 0.68 us
  local copies, waits for them, and re-layouts: 4.5 us -> 0.01 us
  matrix products: 2.9 us -> 0 us
  other arithmetic: 3.95 us -> 1.69 us
    reduce_scatter x1 -> x0, waiting for transfers between devices: 36.3 us -> none  [on_device(): lax.psum_scatter(partial_value, 'red', scatter_dimension=0, tiled=True)]
    pallas_call x0 -> x1, Pallas kernels: none -> 19.8 us  [on_device(): pl.pallas_call(functools.partial(kernel, whole), out_shape=jax.ShapeDtype...]
    all_gather x1 -> x0, blocking collectives: 15.5 us -> none  [on_device(): every_tile = lax.all_gather(amplitudes, 'owner', axis=0, tiled=True)]
    all_gather x1 -> x0, waiting for transfers between devices: 6.57 us -> none  [on_device(): gathered_integrals = lax.all_gather(integrals, 'slab', axis=0, tiled=True)]
    gather x3 -> x0, local copies, waits for them, and re-layouts: 3.22 us -> none  [the longest x1 1.97 us: accumulate(): jnp.take(gathered_integrals, integral_block, axis=0)]
    dot_general x1 -> x0, matrix products: 2.9 us -> none  [accumulate(): jnp.einsum('qkac,qkcx->qax', integral_rows, amplitude_rows, preferred_ele...]
    broadcast_in_dim x3 -> x0, local copies, waits for them, and re-layouts: 1.28 us -> none  [the longest x1 1.12 us: on_device(): initial = jnp.zeros((group_tiles, tile_rows, tile_columns), jnp.float32)]
  transfers between devices with their start and end apart: 2 -> 0, of which waited for: 2 -> 0; matrix products, arithmetic and copies ran while one was open for 2% -> 0% of each run, Pallas kernels for 0% -> 0%
where the time goes in v1:
time: 22.3 us; the launch traced here: 22.1 us
  Pallas kernels  19.8 us (89%)
  other arithmetic  1.69 us (8%)
  between operations  0.68 us (3%)
    pallas_call x1, Pallas kernels, on_device(): pl.pallas_call(functools.partial(kernel, whole), out_shape=jax.ShapeDtype...  19.8 us
    div x1, other arithmetic, on_device(): return residual / denominators  1.69 us

profile of v1, /device:TPU:1, one launch (start us, length us, event | category | flops | bytes accessed | tf_op | source)
XLA Modules:
  0.0 22.1 jit_solution(6698014227921048947)
XLA Ops:
  0.7 0.0 copy-start
  0.7 19.8 %gather_contract.1 = f32[2,128,256]{2,1,0:T(8,128)} custom-call(bf16[2,128,256]{2,1,0:T(8,128)(2,1)} %amp_hbm.1, bf16[16,128,128]{2,1,0:T(8,128)(2,1)} %int_hbm.1, s32[1,4]{1,0:T(1,128)} %bitcast.7, s32[8,12]{1,0:T(8,128)} %bitcast.5, s32[8,12]{1,0:T(8,128)} %bitcast.6, s32[1,1]{1,0:T(1,128)} %bitcast.4.live_hbm), custom_call_target="tpu_custom_call" | custom-call | tf_op jit(solution)/shard_map/gather_contract/pallas_call | solution.py:290
  20.4 0.0 copy-done
  20.4 1.7 %div.3 = f32[2,128,256]{2,1,0:T(8,128)} divide(f32[2,128,256]{2,1,0:T(8,128)} %gather_contract.1, f32[2,128,256]{2,1,0:T(8,128)S(1)} %copy-done) | non-fusion elementwise | flops 65536 | bytes 786432 | tf_op jit(solution)/shard_map/div | solution.py:306
Async XLA Ops:
  0.7 19.8 %copy-start = (f32[2,128,256]{2,1,0:T(8,128)S(1)}, f32[2,128,256]{2,1,0:T(8,128)}, u32[]{:S(2)}) copy-start(f32[2,128,256]{2,1,0:T(8,128)} %param.13) | copy-start | bytes 786436

commit v2 on v1

--- a/solution.py
+++ b/solution.py
@@ -62,8 +62,12 @@
     def is_near(q):
         return jnp.abs(q - o) == 1
 
-    def is_far(q):
-        return jnp.abs(q - o) > 1
+    def each_far(act, nearest_first=True):
+        distances = range(2, owners)
+        for d in distances if nearest_first else reversed(distances):
+            for q, inside in ((o - d, o >= d), (o + d, o + d < owners)):
+                q = jnp.clip(q, 0, owners - 1)
+                pl.when(inside)(functools.partial(act, q))
 
     for q in range(owners):
         @pl.when(q != o)
@@ -120,14 +124,11 @@
     to_smem.start()
     spread(o)
     to_smem.wait()
-    for q in range(owners):
-        @pl.when(is_far(q))
-        def _():
-            stage[q] = mine[req_s[q, 0, o]]
-    for q in range(owners):
-        @pl.when(is_far(q))
-        def _():
-            rcopy(stage.at[q], own.at[o], z_send.at[q], z_recv.at[o], owner=q).start()
+    def select(q):
+        stage[q] = mine[req_s[q, 0, o]]
+
+    each_far(select, nearest_first=False)
+    each_far(lambda q: rcopy(stage.at[q], own.at[o], z_send.at[q], z_recv.at[o], owner=q).start(), nearest_first=False)
 
     for d in range(1, reds):
         for t, ref in enumerate(tables):
@@ -166,11 +167,11 @@
         def _():
             forward(p)
 
-    for p in range(owners):
-        @pl.when(is_far(p))
-        def _():
-            rcopy(stage.at[p], own.at[p], z_send.at[p], z_recv.at[p], owner=p).wait_recv()
-            spread(p)
+    def pulled_far(p):
+        rcopy(stage.at[p], own.at[p], z_send.at[p], z_recv.at[p], owner=p).wait_recv()
+        spread(p)
+
+    each_far(pulled_far)
 
     for copy in table_copies:
         copy.wait()
@@ -199,10 +200,7 @@
 
     contract(r, own, True)
 
-    for p in range(owners):
-        @pl.when(is_far(p))
-        def _():
-            forward(p)
+    each_far(forward)
     for p in range(owners):
         rcopy(own.at[p], part.at[p], part_send.at[p], part_recv.at[p], red=mate).wait_recv()
     contract(mate, part, False)
@@ -215,11 +213,8 @@
         contract(there * CORES + (1 - core), far[2 * (dx - 1) + 1], False)
 
     to_neighbours(lambda copy: copy.wait_send())
+    each_far(lambda q: rcopy(stage.at[q], own.at[o], z_send.at[q], z_recv.at[o], owner=q).wait_send())
     for q in range(owners):
-        @pl.when(is_far(q))
-        def _():
-            rcopy(stage.at[q], own.at[o], z_send.at[q], z_recv.at[o], owner=q).wait_send()
-
         @pl.when(q != o)
         def _():
             rcopy(req_v.at[o], req_v.at[o], req_send.at[q], req_recv.at[o], owner=q).wait_send()

time: 22.3 us -> 22.3 us (level)
  no operation moved by 1% of the time
where the time goes in v2:
time: 22.3 us; the launch traced here: 22.1 us
  Pallas kernels  19.8 us (89%)
  other arithmetic  1.69 us (8%)
  between operations  0.68 us (3%)
    pallas_call x1, Pallas kernels, on_device(): pl.pallas_call(functools.partial(kernel, whole), out_shape=jax.ShapeDtype...  19.8 us
    div x1, other arithmetic, on_device(): return residual / denominators  1.69 us

profile of v2, /device:TPU:1, one launch (start us, length us, event | category | flops | bytes accessed | tf_op | source)
XLA Modules:
  0.0 22.1 jit_solution(7217639951213173920)
XLA Ops:
  0.7 0.0 copy-start
  0.7 19.8 %gather_contract.1 = f32[2,128,256]{2,1,0:T(8,128)} custom-call(bf16[2,128,256]{2,1,0:T(8,128)(2,1)} %amp_hbm.1, bf16[16,128,128]{2,1,0:T(8,128)(2,1)} %int_hbm.1, s32[1,4]{1,0:T(1,128)} %bitcast.7, s32[8,12]{1,0:T(8,128)} %bitcast.5, s32[8,12]{1,0:T(8,128)} %bitcast.6, s32[1,1]{1,0:T(1,128)} %bitcast.4.live_hbm), custom_call_target="tpu_custom_call" | custom-call | tf_op jit(solution)/shard_map/gather_contract/pallas_call | solution.py:285
  20.4 0.0 copy-done
  20.4 1.7 %div.3 = f32[2,128,256]{2,1,0:T(8,128)} divide(f32[2,128,256]{2,1,0:T(8,128)} %gather_contract.1, f32[2,128,256]{2,1,0:T(8,128)S(1)} %copy-done) | non-fusion elementwise | flops 65536 | bytes 786432 | tf_op jit(solution)/shard_map/div | solution.py:301
Async XLA Ops:
  0.7 19.8 %copy-start = (f32[2,128,256]{2,1,0:T(8,128)S(1)}, f32[2,128,256]{2,1,0:T(8,128)}, u32[]{:S(2)}) copy-start(f32[2,128,256]{2,1,0:T(8,128)} %param.13) | copy-start | bytes 786436
